TPU v7x, 16 devices: a 4x2x1 block of a 4x4x8 slice. The times are simulated.
16 devices in a mesh: dp: 2 (over y, z), tp: 8 (over x, core).
Axes of the slice: x: 4, y: 2, z: 1, core: 2. Of those that a mesh axis runs over, the one named last changes fastest.
The devices are a block of a 4x4x8 slice.
Arguments:
- x_seq: bfloat16 [8, 2048, 4096], P('dp', 'tp'), parts along dimension 0
- ln_gain: float32 [4096], replicated
- ln_bias: float32 [4096], replicated
- w_qkv: bfloat16 [4096, 16, 3, 256], P(None, 'tp')
- w_out: bfloat16 [4096, 4096], P('tp')
- w_up: bfloat16 [4096, 16384], P(None, 'tp')
- w_down: bfloat16 [16384, 4096], P('tp')
Outputs:
- output: bfloat16 [8, 2048, 4096], P('dp', 'tp'), parts along dimension 0
There are 2 independent parts. A program takes and returns all parts, laid end to end along the dimension named above; an argument that names none is the same for every part.
All inputs are finite; a program needn't handle non-finite values.
Results may differ from a plain program's by a relative error of at most 0.011671.
Values are sent between devices in bfloat16 or wider.
A program may use at most 768 MiB of HBM per device.

v0:
```python
import jax
import jax.numpy as jnp
from jax import lax
from jax.sharding import PartitionSpec as P, NamedSharding

LN_EPS = 1e-5


def layer_norm(x_f32, ln_gain, ln_bias):
    row_mean = jnp.mean(x_f32, axis=-1, keepdims=True)
    centered = x_f32 - row_mean
    variance = jnp.mean(centered * centered, axis=-1, keepdims=True)
    return centered * lax.rsqrt(variance + LN_EPS) * ln_gain + ln_bias


def solution(mesh):
    def local_layer(x_blk, ln_gain, ln_bias, w_qkv, w_out, w_up, w_down):
        x_full = lax.all_gather(x_blk, "tp", axis=1, tiled=True)
        seq_len = x_full.shape[1]
        model_dim = x_full.shape[2]
        kv_local, group_width, head_dim = w_qkv.shape[1:]
        group_q = group_width - 2
        normed = layer_norm(x_full.astype(jnp.float32), ln_gain, ln_bias).astype(jnp.bfloat16)
        proj_qkv = jnp.einsum("bsd,dgjh->bsgjh", normed, w_qkv,
                              preferred_element_type=jnp.float32).astype(jnp.bfloat16)
        queries = proj_qkv[:, :, :, :group_q]
        key_rows = proj_qkv[:, :, :, group_q]
        value_rows = proj_qkv[:, :, :, group_q + 1]
        scores = jnp.einsum("bsgjh,btgh->bgjst", queries, key_rows,
                            preferred_element_type=jnp.float32) * (head_dim ** -0.5)
        causal = (lax.broadcasted_iota(jnp.int32, (seq_len, seq_len), 0)
                  >= lax.broadcasted_iota(jnp.int32, (seq_len, seq_len), 1))
        scores = jnp.where(causal, scores, -jnp.inf)
        attn_prob = jax.nn.softmax(scores, axis=-1).astype(jnp.bfloat16)
        context = jnp.einsum("bgjst,btgh->bgjsh", attn_prob, value_rows,
                             preferred_element_type=jnp.float32).astype(jnp.bfloat16)
        w_heads = w_out.reshape(kv_local, group_q, head_dim, model_dim)
        attn_part = jnp.einsum("bgjsh,gjhd->bsd", context, w_heads, preferred_element_type=jnp.float32)
        hidden = jnp.einsum("bsd,df->bsf", normed, w_up, preferred_element_type=jnp.float32)
        activated = jax.nn.gelu(hidden, approximate=False).astype(jnp.bfloat16)
        mlp_part = jnp.einsum("bsf,fd->bsd", activated, w_down, preferred_element_type=jnp.float32)
        branch_part = (attn_part + mlp_part).astype(jnp.bfloat16)
        branch = lax.psum_scatter(branch_part, "tp", scatter_dimension=1, tiled=True)
        return (x_blk.astype(jnp.float32) + branch.astype(jnp.float32)).astype(jnp.bfloat16)

    return jax.shard_map(
        local_layer, mesh=mesh,
        in_specs=(P("dp", "tp", None), P(), P(), P(None, "tp", None, None),
                  P("tp", None), P(None, "tp"), P("tp", None)),
        out_specs=P("dp", "tp", None), check_vma=False)
```

profile of v0, /device:TPU:112, one launch (start us, length us, event | category | flops | bytes accessed | tf_op | source)
XLA Modules:
  0.0 1515.7 jit_solution(5002368537073073952)
XLA Ops:
  6.5 0.0 all-gather.2.cloned.1.call-start
  6.6 0.7 all-gather.2.cloned.1.call-update
  7.3 0.1 reduce-scatter.2.cloned.1.call-start
  7.4 4.1 iota_compare_fusion
  11.4 0.0 copy-start.4
  11.4 0.0 copy-start.6
  11.5 293.6 %all-gather.2.cloned.1.call-done = bf16[4,2048,4096]{2,1,0:T(8,128)(2,1)} async-done(((bf16[4,256,4096]{2,1,0:T(8,128)(2,1)}), bf16[4,2048,4096]{2,1,0:T(8,128)(2,1)}) %all-gather.2.cloned.1.call-update) | async-done | bytes 67108880 | tf_op jit(solution)/shard_map/all_gather | solution.py:18
  305.1 20.8 %convert_reduce_fusion = f32[4,2048]{1,0:T(4,128)S(1)} fusion(bf16[4,2048,4096]{2,1,0:T(8,128)(2,1)} %all-gather.2.cloned.1.call-done), kind=kLoop, calls=%fused_computation.1 | loop fusion | flops 67100672 | bytes 67141632 | tf_op jit(solution)/shard_map/reduce_sum | solution.py:10
  325.9 0.0 copy-start
  325.9 24.2 %fusion.2 = f32[4,2048]{1,0:T(4,128)S(1)} fusion(bf16[4,2048,4096]{2,1,0:T(8,128)(2,1)} %all-gather.2.cloned.1.call-done, f32[4,2048]{1,0:T(4,128)S(1)} %broadcast_multiply_fusion), kind=kLoop, calls=%fused_computation.4 | loop fusion | flops 134209536 | bytes 67174400 | tf_op jit(solution)/shard_map/reduce_sum | solution.py:12
  350.1 0.0 copy-done
  350.1 0.0 copy-start.2
  350.1 0.6 copy-done.2
  350.7 0.0 copy-done.4
  350.7 0.0 copy-done.6
  350.7 116.5 %fusion.61 = bf16[4,2048,2,3,256]{4,1,3,2,0:T(8,128)(2,1)} fusion(f32[4096]{0:T(1024)S(1)} %copy-done.4, f32[4096]{0:T(1024)S(1)} %copy-done.6, f32[4,2048]{1,0:T(4,128)S(1)} %add_rsqrt_fusion, f32[4,2048]{1,0:T(4,128)S(1)} %broadcast_multiply_fusion, bf16[4,2048,4096]{2,1,0:T(8,128)(2,1)} %all-gather.2.cloned.1.call-done, bf16[4096,2,3,256]{3,1,2,0:T(2,128)(2,1)} %param.10), kind=kOutput, calls=%fused_computation.79 | convolution fusion | flops 103293124608 | bytes 104955904 | tf_op jit(solution)/shard_map/bsd,dgjh->bsgjh/dot_general | solution.py:24
  467.3 54.7 %fusion.8 = (f32[4,2,2048]{2,1,0:T(2,128)S(1)}, f32[4,2,2048,2048]{3,2,1,0:T(8,128)}) fusion(pred[2048,2048]{0,1:T(8,128)(4,1)} %iota_compare_fusion, bf16[4,2048,2,3,256]{4,1,3,2,0:T(8,128)(2,1)} %fusion.61), kind=kOutput, calls=%fused_computation.14 | convolution fusion | flops 17280516096 | bytes 155254784 | tf_op jit(solution)/shard_map/bsgjh,btgh->bgjst/dot_general | solution.py:29
  522.0 42.4 %fusion.7 = f32[4,2,2048]{2,1,0:T(2,128)S(1)} fusion(f32[4,2,2048,2048]{3,2,1,0:T(8,128)} %get-tuple-element.8, f32[4,2,2048]{2,1,0:T(2,128)S(1)} %get-tuple-element.7, pred[2048,2048]{0,1:T(8,128)(4,1)} %iota_compare_fusion), kind=kLoop, calls=%fused_computation.13 | loop fusion | flops 134201344 | bytes 138543104 | tf_op jit(solution)/shard_map/reduce_sum | solution.py:34
  564.4 63.9 %fusion.123 = bf16[4,2,2048,256]{3,2,1,0:T(8,128)(2,1)} fusion(bf16[4,2048,2,3,256]{4,1,3,2,0:T(8,128)(2,1)} %fusion.61, f32[4,2,2048]{2,1,0:T(2,128)S(1)} %fusion.7, f32[4,2,2048]{2,1,0:T(2,128)S(1)} %get-tuple-element.7, f32[4,2,2048,2048]{3,2,1,0:T(8,128)} %get-tuple-element.8, pred[2048,2048]{0,1:T(8,128)(4,1)} %iota_compare_fusion), kind=kOutput, calls=%fused_computation.89.clone.1 | convolution fusion | flops 17351835648 | bytes 155320320 | tf_op jit(solution)/shard_map/bgjst,btgh->bgjsh/dot_general | solution.py:35
  628.4 0.0 copy-start.1
  628.4 0.0 copy-start.3
  628.4 0.0 copy-start.5
  628.4 0.0 copy-start.7
  628.4 52.6 %fusion.69 = f32[4,2048,4096,1]{2,1,3,0:T(8,128)} fusion(bf16[2,256,4096,1]{2,1,0,3:T(8,128)(2,1)} %bitcast.93, bf16[4,2,2048,256]{3,2,1,0:T(8,128)(2,1)} %fusion.123), kind=kOutput, calls=%fused_computation.88 | convolution fusion | flops 34359738368 | bytes 146800640 | tf_op jit(solution)/shard_map/bgjsh,gjhd->bsd/dot_general | solution.py:38
  681.0 0.0 copy-done.1
  681.0 0.0 copy-done.3
  681.0 0.0 copy-done.5
  681.0 0.0 copy-done.7
  681.0 196.6 %fusion.60 = (u8[2048,2048]{1,0:T(8,128)(4,1)}, u8[2048,2048]{1,0:T(8,128)(4,1)}, f32[4,2048,2048]{2,1,0:T(8,128)}) fusion(bf16[4096,2048]{1,0:T(8,128)(2,1)} %param.12, bf16[4,2048,4096]{2,1,0:T(8,128)(2,1)} %all-gather.2.cloned.1.call-done, f32[4096]{0:T(1024)S(1)} %copy-done.5, f32[4096]{0:T(1024)S(1)} %copy-done.7, f32[4,2048]{1,0:T(4,128)S(1)} %copy-done.3, ...), kind=kOutput, calls=%fused_computation.78 | convolution fusion | flops 137849995264 | bytes 159481856 | tf_op jit(solution)/shard_map/bsd,df->bsf/dot_general | solution.py:39
  877.6 296.4 %fusion.6 = bf16[4,2048,4096]{2,1,0:T(8,128)(2,1)} fusion(f32[4,2048,4096,1]{2,1,3,0:T(8,128)} %fusion.69, f32[4,2048,2048]{2,1,0:T(8,128)} %get-tuple-element.9, bf16[2048,4096]{1,0:T(8,128)(2,1)} %param.13, u8[2048,2048]{1,0:T(8,128)(4,1)} %get-tuple-element.6, u8[2048,2048]{1,0:T(8,128)(4,1)} %get-tuple-element.5), kind=kOutput, calls=%fused_computation.10 | convolution fusion | flops 138680467456 | bytes 293601280 | tf_op jit(solution)/shard_map/bsf,fd->bsd/dot_general | solution.py:41
  1173.9 0.1 reduce-scatter.2.cloned.1.call-update
  1174.0 324.3 %reduce-scatter.2.cloned.1.call-done = bf16[4,256,4096]{2,1,0:T(8,128)(2,1)} async-done(((bf16[4,2048,4096]{2,1,0:T(8,128)(2,1)}), bf16[4,256,4096]{2,1,0:T(8,128)(2,1)}) %reduce-scatter.2.cloned.1.call-update) | async-done | bytes 8388624 | tf_op jit(solution)/shard_map/reduce_scatter | solution.py:43
  1498.3 10.1 add_convert_fusion
  (2 shorter events, 0.0 us)
Async XLA Ops:
  6.5 298.5 %all-gather.2.cloned.1.call-start = ((), (), s32[]{:S(2)}) async-start(), calls=%async_computation.1 | async-start | bytes 75497472 | tf_op jit(solution)/shard_map/all_gather | solution.py:18
  7.3 1491.0 %reduce-scatter.2.cloned.1.call-start = ((), (), s32[]{:S(2)}) async-start(), calls=%async_computation.2 | async-start | bytes 75497472 | tf_op jit(solution)/shard_map/reduce_scatter | solution.py:43
  11.4 339.3 %copy-start.4 = (f32[4096]{0:T(1024)S(1)}, f32[4096]{0:T(1024)}, u32[]{:S(2)}) copy-start(f32[4096]{0:T(1024)} %param.9) | copy-start | bytes 49156
  11.4 339.3 %copy-start.6 = (f32[4096]{0:T(1024)S(1)}, f32[4096]{0:T(1024)}, u32[]{:S(2)}) copy-start(f32[4096]{0:T(1024)} %param.8) | copy-start | bytes 49156
  325.9 24.3 %copy-start = (f32[4,2048]{1,0:T(4,128)}, f32[4,2048]{1,0:T(4,128)S(1)}, u32[]{:S(2)}) copy-start(f32[4,2048]{1,0:T(4,128)S(1)} %broadcast_multiply_fusion) | copy-start | bytes 98308
  350.1 0.6 copy-start.2
  628.4 52.6 %copy-start.1 = (f32[4,2048]{1,0:T(4,128)S(1)}, f32[4,2048]{1,0:T(4,128)}, u32[]{:S(2)}) copy-start(f32[4,2048]{1,0:T(4,128)} %copy-done) | copy-start | bytes 98308
  628.4 52.6 %copy-start.3 = (f32[4,2048]{1,0:T(4,128)S(1)}, f32[4,2048]{1,0:T(4,128)}, u32[]{:S(2)}) copy-start(f32[4,2048]{1,0:T(4,128)} %copy-done.2) | copy-start | bytes 98308
  628.4 52.6 %copy-start.5 = (f32[4096]{0:T(1024)S(1)}, f32[4096]{0:T(1024)}, u32[]{:S(2)}) copy-start(f32[4096]{0:T(1024)} %param.9) | copy-start | bytes 49156
  628.4 52.6 %copy-start.7 = (f32[4096]{0:T(1024)S(1)}, f32[4096]{0:T(1024)}, u32[]{:S(2)}) copy-start(f32[4096]{0:T(1024)} %param.8) | copy-start | bytes 49156
Sparse Core Ops, SparseCore 0:
  8.9 296.0 all-gather.1
  1174.1 324.1 reduce-scatter.1
where the time goes:
time: 1530 us; the launch traced here: 1520 us
  matrix products  781 us (51%)
  waiting for transfers between devices  619 us (40%)
  other arithmetic  102 us (7%)
    reduce_scatter x1, waiting for transfers between devices, local_layer(): lax.psum_scatter(branch_part, 'tp', scatter_dimension=1, tiled=True)  324 us
    dot_general x1, matrix products, local_layer(): jnp.einsum('bsf,fd->bsd', activated, w_down, preferred_element_type=jnp.f...  296 us
    all_gather x1, waiting for transfers between devices, local_layer(): x_full = lax.all_gather(x_blk, 'tp', axis=1, tiled=True)  294 us
    dot_general x1, matrix products, local_layer(): jnp.einsum('bsd,df->bsf', normed, w_up, preferred_element_type=jnp.float32)  197 us
    dot_general x1, matrix products, local_layer(): jnp.einsum('bsd,dgjh->bsgjh', normed, w_qkv, preferred_element_type=jnp.f...  117 us
    dot_general x1, matrix products, local_layer(): jnp.einsum('bgjst,btgh->bgjsh', attn_prob, value_rows, preferred_element_...  63.9 us
    dot_general x1, matrix products, local_layer(): jnp.einsum('bsgjh,btgh->bgjst', queries, key_rows, preferred_element_type...  54.7 us
    dot_general x1, matrix products, local_layer(): jnp.einsum('bgjsh,gjhd->bsd', context, w_heads, preferred_element_type=jn...  52.6 us
  transfers between devices with their start and end apart: 2, of which 2 were waited for; matrix products, arithmetic and copies ran while one was open for 0% of the time, Pallas kernels for 0%

commit v1 on v0

v1 whole, which is shorter than its diff:
```python
import functools

import jax
import jax.numpy as jnp
from jax import lax
from jax.experimental import pallas as pl
from jax.experimental.pallas import tpu as pltpu
from jax.sharding import PartitionSpec as P

LN_EPS = 1e-5
NJ = 4


def layer_kernel(x_ref, gain_ref, bias_ref, wqkv_hbm, wout_hbm, wup_hbm, wdown_hbm,
                 own_out, left_out, right_out, n_all, ho, pbuf, pout, tin,
                 wqkv, wup, wdo, gain, bias,
                 ag_is, ag_ir, ag_ds, ag_dr, p_s, p_r, t_s, t_r, m_s, m_r,
                 w_sem, v_sem, ln_sem, a_sem, h_sem, o_sem, d_sem, pb_sem, os_sem, f_sem):
    batch, rows, dim = x_ref.shape
    half = rows // 2
    ff = wup.shape[1]
    attn = wdo.shape[0] - ff
    qkv_cols = wqkv.shape[1]
    n_heads = 2
    head = attn // n_heads
    n_chips = n_all.shape[1]
    seq = n_chips * 2 * rows
    ncol = dim // NJ
    f32, bf16 = jnp.float32, jnp.bfloat16

    me = lax.axis_index("tp")
    chip, core = me // 2, me % 2
    other = 1 - core
    partner = chip * 2 + other
    right = ((chip + 1) % n_chips) * 2 + core
    left = ((chip + n_chips - 1) % n_chips) * 2 + core

    def remote(src, dst, send, recv, dev):
        return pltpu.make_async_remote_copy(
            src_ref=src, dst_ref=dst, send_sem=send, recv_sem=recv,
            device_id={"tp": dev}, device_id_type=pl.DeviceIdType.MESH)

    barrier = pltpu.get_barrier_semaphore()
    for dev in (partner, right, left):
        pl.semaphore_signal(barrier, inc=1, device_id={"tp": dev}, device_id_type=pl.DeviceIdType.MESH)
    pl.semaphore_wait(barrier, 3)

    w_copies = (
        pltpu.make_async_copy(wqkv_hbm, wqkv, w_sem.at[0]),
        pltpu.make_async_copy(wup_hbm, wup, w_sem.at[1]),
        pltpu.make_async_copy(wdown_hbm, wdo.at[pl.ds(0, ff)], w_sem.at[2]),
        pltpu.make_async_copy(wout_hbm, wdo.at[pl.ds(ff, attn)], w_sem.at[3]),
    )
    v_copies = (pltpu.make_async_copy(gain_ref, gain, v_sem.at[0]),
                pltpu.make_async_copy(bias_ref, bias, v_sem.at[1]))
    for cp in v_copies:
        cp.start()

    def unit(u):
        g, b = u // 2, u % 2
        near = (g * (3 - g)) // 2
        off = near * (2 * b - 1) + 2 * (g // 3)
        hf = (b + near * (g - 1)) % 2
        return (chip + off + n_chips) % n_chips, hf

    def piece(s, d, hf, k):
        return n_all.at[s, d, hf, pl.ds(pl.multiple_of(k * half, half), half)]

    def ici_copy(s, u, d, hf, dev):
        return remote(piece(s, d, hf, core), piece(s, d, hf, core), ag_is.at[s, u], ag_ir.at[s, u], dev)

    def d2d_copy(s, u, d, hf, k):
        return remote(piece(s, d, hf, k), piece(s, d, hf, k), ag_ds.at[s, u], ag_dr.at[s, u], partner)

    def ag_send(s, buf):
        part, step = rows // 4, 32

        def load(q):
            at = pl.ds(q * part, part)
            return pltpu.make_async_copy(x_ref.at[s, at], buf.at[at], ln_sem.at[0, q])

        def store(q):
            dst = n_all.at[s, chip, q // 2, pl.ds(pl.multiple_of(core * half + (q % 2) * part, part), part)]
            return pltpu.make_async_copy(buf.at[pl.ds(q * part, part)], dst, ln_sem.at[1, q])

        for q in range(4):
            load(q).start()
        for q in range(4):
            load(q).wait()

            @pl.loop(0, part // step)
            def _(r):
                at = pl.ds(pl.multiple_of(q * part + r * step, step), step)
                v = buf[at, :].astype(f32)
                mean = jnp.mean(v, axis=-1, keepdims=True)
                cen = v - mean
                var = jnp.mean(cen * cen, axis=-1, keepdims=True)
                buf[at, :] = (cen * lax.rsqrt(var + LN_EPS) * gain[...] + bias[...]).astype(bf16)
            store(q).start()
        for q in range(4):
            store(q).wait()
        ici_copy(s, 2, chip, 0, right).start()
        ici_copy(s, 3, chip, 1, left).start()
        d2d_copy(s, 0, chip, 0, core).start()
        d2d_copy(s, 1, chip, 1, core).start()
        ici_copy(s, 4, chip, 1, right).start()
        ici_copy(s, 5, chip, 0, left).start()

    def forward(s, us):
        for u in us:
            d, hf = unit(u)
            ici_copy(s, u, d, hf, right).wait_recv()
            if u == 2:
                ici_copy(s, 6, d, hf, right).start()
            if u == 3:
                ici_copy(s, 7, d, hf, left).start()
            d2d_copy(s, u, d, hf, core).start()

    def dest(i):
        is2 = (i * (i - 1) * (3 - i) * (4 - i)) // 4
        is3 = (i * (i - 1) * (i - 2) * (4 - i)) // 6
        return (chip + 2 - i + 3 * is2 + is3 + n_chips) % n_chips

    def cols(j):
        return pl.ds(pl.multiple_of(j * ncol, ncol), ncol)

    def to_right(s, ii, j):
        return remote(pout.at[s, ii, :, cols(j)], left_out.at[s, :, cols(j)], m_s.at[s, j], m_r.at[s, j], right)

    def to_left(s, ii, j):
        return remote(pout.at[s, ii, :, cols(j)], right_out.at[s, :, cols(j)], m_s.at[s, NJ + j], m_r.at[s, NJ + j],
                      left)

    def transit(s, j, dev):
        return remote(pout.at[s, 0, :, cols(j)], tin.at[s, :, cols(j)], t_s.at[s, j], t_r.at[s, j], dev)

    def relay(s):
        def scope(a, b):
            def loads(j):
                return (pltpu.make_async_copy(pout.at[s, 1 + j // 2, :, cols(j)], a.at[j % 2], f_sem.at[0, j % 2]),
                        pltpu.make_async_copy(tin.at[s, :, cols(j)], b.at[j % 2], f_sem.at[1, j % 2]))

            def store(j):
                return pltpu.make_async_copy(a.at[j % 2], pout.at[s, 1 + j // 2, :, cols(j)], f_sem.at[2, j % 2])

            def send(j):
                return to_right(s, 1, j) if j < NJ // 2 else to_left(s, 2, j)

            order = tuple(range(NJ))
            for n, j in enumerate(order):
                if n == 0:
                    transit(s, j, right).wait_recv()
                    for cp in loads(j):
                        cp.start()
                if n >= 1:
                    store(order[n - 1]).wait()
                    send(order[n - 1]).start()
                if n + 1 < NJ:
                    transit(s, order[n + 1], right).wait_recv()
                    for cp in loads(order[n + 1]):
                        cp.start()
                for cp in loads(j):
                    cp.wait()
                step = 64

                @pl.loop(0, rows // step)
                def _(r):
                    at = pl.ds(pl.multiple_of(r * step, step), step)
                    a[j % 2, at, :] = (a[j % 2, at, :].astype(f32) + b[j % 2, at, :].astype(f32)).astype(bf16)
                store(j).start()
            store(order[-1]).wait()
            send(order[-1]).start()
        pl.run_scoped(scope, pltpu.VMEM((2, rows, ncol), bf16), pltpu.VMEM((2, rows, ncol), bf16))

    def phase_a(s, qkv):
        def scope(nbuf, hbuf):
            def load(u):
                d, hf = unit(u)
                return pltpu.make_async_copy(n_all.at[s, d, hf], nbuf.at[u % 2], a_sem.at[u % 2])

            def arrived(u):
                d, hf = unit(u)
                d2d_copy(s, u, d, hf, other).wait_recv()

            def hstore(u, k):
                d, hf = unit(u)
                return pltpu.make_async_copy(
                    hbuf.at[u % 2, pl.ds(k * half, half)],
                    ho.at[2 * d + k, pl.ds(pl.multiple_of(hf * half, half), half), pl.ds(0, ff)],
                    h_sem.at[u % 2, k])

            arrived(0)
            load(0).start()

            @pl.loop(0, 2 * n_chips)
            def _(u):
                load(u).wait()

                @pl.when(jnp.logical_and(s > 0, u == 3))
                def _():
                    forward(s, (6, 7))

                @pl.when(jnp.logical_and(s > 0, u < 7))
                def _():
                    arrived(u + 1)
                    load(u + 1).start()

                @pl.when(u >= 2)
                def _():
                    for k in range(2):
                        hstore(u - 2, k).wait()

                @pl.when(jnp.logical_and(s == 0, u == 0))
                def _():
                    w_copies[0].wait()
                    w_copies[1].wait()

                d, hf = unit(u)
                slot = u % 2
                r = jnp.dot(nbuf[slot], wqkv[...], preferred_element_type=f32).astype(bf16)
                for k in range(2):
                    pos = pl.multiple_of(d * (2 * rows) + k * rows + hf * half, half)
                    qkv[pl.ds(pos, half), :] = r[k * half:(k + 1) * half]
                h = jnp.dot(nbuf[slot], wup[...], preferred_element_type=f32)
                hbuf[slot] = (0.5 * h * (1.0 + lax.erf(h * (2.0 ** -0.5)))).astype(bf16)
                for k in range(2):
                    hstore(u, k).start()

                @pl.when(s == 0)
                def _():
                    @pl.when(u == 1)
                    def _():
                        forward(0, (2, 3))
                        ag_send(1, nbuf.at[0])

                    @pl.when(u == 3)
                    def _():
                        forward(0, (4, 5))

                    @pl.when(u == 5)
                    def _():
                        forward(0, (6, 7))

                    @pl.when(u < 7)
                    def _():
                        arrived(u + 1)
                        load(u + 1).start()

            for u in (6, 7):
                for k in range(2):
                    hstore(u, k).wait()
        pl.run_scoped(scope, pltpu.VMEM((2, rows, dim), bf16), pltpu.VMEM((2, rows, ff), bf16))

    def phase_b(qkv):
        def ostore(t):
            return pltpu.make_async_copy(qkv.at[pl.ds(t * rows, rows), pl.ds(0, attn)],
                                         ho.at[t, :, pl.ds(ff, attn)], o_sem.at[t])
        scale = head ** -0.5

        def scope(scores, probs):
            keep = (lax.broadcasted_iota(jnp.int32, (rows, rows), 0)
                    >= lax.broadcasted_iota(jnp.int32, (rows, rows), 1))
            for t in range(seq // rows):
                r0, n = t * rows, (t + 1) * rows
                tops = []
                for h in range(n_heads):
                    q = qkv[r0:r0 + rows, h * head:(h + 1) * head]
                    k = qkv[0:n, attn + h * head:attn + (h + 1) * head]
                    sc = lax.dot_general(q, k, (((1,), (1,)), ((), ())), preferred_element_type=f32)
                    diag = jnp.where(keep, sc[:, n - rows:], -jnp.inf)
                    top = jnp.max(diag, axis=1, keepdims=True)
                    if t:
                        scores[h, :, 0:n - rows] = sc[:, :n - rows]
                        top = jnp.maximum(top, jnp.max(sc[:, :n - rows], axis=1, keepdims=True))
                    scores[h, :, n - rows:n] = diag
                    tops.append(top)
                for h in range(n_heads):
                    v = qkv[0:n, 2 * attn + h * head:2 * attn + (h + 1) * head]
                    total = jnp.zeros((rows, 1), f32)
                    for c in range(0, n, rows):
                        e = jnp.exp((scores[h, :, c:c + rows] - tops[h]) * scale)
                        scores[h, :, c:c + rows] = e
                        total = total + jnp.sum(e, axis=1, keepdims=True)
                    inverse = 1.0 / total
                    for c in range(0, n, rows):
                        probs[h, :, c:c + rows] = (scores[h, :, c:c + rows] * inverse).astype(bf16)
                    o = jnp.dot(probs[h, :, 0:n], v, preferred_element_type=f32)
                    qkv[r0:r0 + rows, h * head:(h + 1) * head] = o.astype(bf16)
                if t % 4 == 3:
                    for done in range(t - 3, t + 1):
                        ostore(done).start()
            for t in range(seq // rows):
                ostore(t).wait()
        pl.run_scoped(scope, pltpu.VMEM((n_heads, rows, seq), f32), pltpu.VMEM((n_heads, rows, seq), bf16))

    def phase_d(s):
        def scope(lhs, pst, ost, pb):
            def load_p(i):
                return pltpu.make_async_copy(ho.at[2 * dest(i) + other], lhs.at[i % 2, pl.ds(0, rows)],
                                             d_sem.at[i % 2, 0])

            def load_o(i):
                return pltpu.make_async_copy(ho.at[2 * dest(i - 1) + core], lhs.at[i % 2, pl.ds(rows, rows)],
                                             d_sem.at[i % 2, 1])

            def swap(p):
                return remote(pst.at[p % 2], pbuf.at[s, p // NJ, p % NJ], p_s.at[p % 2], p_r.at[s, p], partner)

            def pb_load(m):
                return pltpu.make_async_copy(pbuf.at[s, m // NJ, m % NJ], pb.at[m % 2], pb_sem.at[m % 2])

            def pb_start(m):
                swap(m).wait_recv()
                pb_load(m).start()

            def ostore(m):
                return pltpu.make_async_copy(ost.at[m % 2], pout.at[s, m // NJ, :, cols(m % NJ)], os_sem.at[m % 2])

            def ostored(m):
                pltpu.make_async_copy(ost.at[m % 2], pout.at[s, 0, :, cols(m % NJ)], os_sem.at[m % 2]).wait()

            def post(m):
                ostored(m)
                ii, j = m // NJ, m % NJ

                @pl.when(jnp.logical_and(ii == 0, j < NJ // 2))
                def _():
                    transit(s, j, right).start()

                @pl.when(jnp.logical_and(ii == 0, j >= NJ // 2))
                def _():
                    transit(s, j, left).start()

                @pl.when(jnp.logical_and(ii == 1, j >= NJ // 2))
                def _():
                    to_right(s, 1, j).start()

                @pl.when(jnp.logical_and(ii == 2, j < NJ // 2))
                def _():
                    to_left(s, 2, j).start()

            load_p(0).start()

            @pl.when(s == 0)
            def _():
                w_copies[2].wait()
                w_copies[3].wait()
            load_p(0).wait()
            load_p(1).start()
            load_o(1).start()

            @pl.loop(0, NJ)
            def _(j):
                @pl.when(j >= 2)
                def _():
                    swap(j - 2).wait_send()

                @pl.when(j == NJ - 1)
                def _():
                    pb_start(0)
                r = jnp.dot(lhs[0, 0:rows], wdo[:, cols(j)], preferred_element_type=f32)
                pst[j % 2] = r.astype(bf16)
                swap(j).start()

            @pl.when(s < batch - 1)
            def _():
                forward(s + 1, (2, 3))

            @pl.loop(0, 3 * NJ)
            def _(m):
                p = m + NJ
                i, j = p // NJ, p % NJ

                @pl.when(j == 0)
                def _():
                    load_p(i).wait()
                    load_o(i).wait()
                    load_o(i + 1).start()

                @pl.when(jnp.logical_and(j == 0, i < 3))
                def _():
                    load_p(i + 1).start()
                swap(p - 2).wait_send()
                pb_load(m).wait()
                pb_start(m + 1)
                r = jnp.dot(lhs[i % 2], wdo[:, cols(j)], preferred_element_type=f32)
                pst[m % 2] = r[:rows].astype(bf16)
                ost[m % 2] = (r[rows:] + pb[m % 2].astype(f32)).astype(bf16)
                swap(p).start()
                ostore(m).start()

                @pl.when(m >= 1)
                def _():
                    post(m - 1)

            @pl.when(s < batch - 1)
            def _():
                forward(s + 1, (4, 5))
            load_o(4).wait()

            @pl.loop(3 * NJ, 4 * NJ)
            def _(m):
                j = m % NJ
                pb_load(m).wait()

                @pl.when(j < NJ - 1)
                def _():
                    pb_start(m + 1)
                r = jnp.dot(lhs[0, rows:], wdo[:, cols(j)], preferred_element_type=f32)
                ost[m % 2] = (r + pb[m % 2].astype(f32)).astype(bf16)
                post(m - 1)
                pltpu.make_async_copy(ost.at[m % 2], own_out.at[s, :, cols(j)], os_sem.at[m % 2]).start()
            ostored(4 * NJ - 1)
            for p in (4 * NJ - 2, 4 * NJ - 1):
                swap(p).wait_send()
        pl.run_scoped(scope, pltpu.VMEM((2, 2 * rows, ff + attn), bf16), pltpu.VMEM((2, rows, ncol), bf16),
                      pltpu.VMEM((2, rows, ncol), bf16), pltpu.VMEM((2, rows, ncol), bf16))

    for cp in v_copies:
        cp.wait()
    pl.run_scoped(functools.partial(ag_send, 0), pltpu.VMEM((rows, dim), bf16))
    for cp in w_copies:
        cp.start()

    @pl.loop(0, batch)
    def _(s):
        def scope(qkv):
            phase_a(s, qkv)

            @pl.when(s > 0)
            def _():
                relay(s - 1)
            phase_b(qkv)
        pl.run_scoped(scope, pltpu.VMEM((seq, qkv_cols), bf16))
        phase_d(s)

        @pl.when(s < batch - 2)
        def _():
            pl.run_scoped(functools.partial(ag_send, s + 2), pltpu.VMEM((rows, dim), bf16))

    relay(batch - 1)

    @pl.loop(0, batch)
    def _(s):
        for j in range(NJ):
            to_right(s, 1, j).wait_recv()
            to_left(s, 2, j).wait_recv()
            to_right(s, 1, j).wait_send()
            to_left(s, 2, j).wait_send()
            transit(s, j, right).wait_send()
        for u in range(2 * n_chips):
            d, hf = unit(u)
            d2d_copy(s, u, d, hf, core).wait_send()
            if u >= 2:
                ici_copy(s, u, d, hf, right).wait_send()


def layer_call(x_blk, ln_gain, ln_bias, wqkv, w_out, w_up, w_down, n_tp):
    batch, rows, dim = x_blk.shape
    ff, attn, qkv_cols = w_up.shape[1], w_out.shape[0], wqkv.shape[1]
    n_chips = n_tp // 2
    ncol = dim // NJ
    bf16 = jnp.bfloat16
    dma = pltpu.SemaphoreType.DMA
    flops = 2 * batch * n_tp * rows * dim * (qkv_cols + 2 * ff + attn)
    outs = pl.pallas_call(
        layer_kernel,
        name="parallel_layer",
        out_shape=[
            jax.ShapeDtypeStruct((batch, rows, dim), bf16),
            jax.ShapeDtypeStruct((batch, rows, dim), bf16),
            jax.ShapeDtypeStruct((batch, rows, dim), bf16),
            jax.ShapeDtypeStruct((batch, n_chips, 2, rows, dim), bf16),
            jax.ShapeDtypeStruct((n_tp, rows, ff + attn), bf16),
            jax.ShapeDtypeStruct((batch, 4, NJ, rows, ncol), bf16),
            jax.ShapeDtypeStruct((batch, 3, rows, dim), bf16),
            jax.ShapeDtypeStruct((batch, rows, dim), bf16),
        ],
        in_specs=[pl.BlockSpec(memory_space=pl.ANY)] * 7,
        out_specs=[pl.BlockSpec(memory_space=pl.ANY)] * 8,
        scratch_shapes=[
            pltpu.VMEM((dim, qkv_cols), bf16), pltpu.VMEM((dim, ff), bf16), pltpu.VMEM((ff + attn, dim), bf16),
            pltpu.VMEM((1, dim), jnp.float32), pltpu.VMEM((1, dim), jnp.float32),
            dma((batch, 8)), dma((batch, 8)), dma((batch, 8)), dma((batch, 8)),
            dma((2,)), dma((batch, 4 * NJ)), dma((batch, NJ)), dma((batch, NJ)),
            dma((batch, 2 * NJ)), dma((batch, 2 * NJ)),
            dma((4,)), dma((2,)), dma((2, 4)), dma((2,)), dma((2, 2)), dma((n_tp,)), dma((2, 2)), dma((2,)), dma((2,)),
            dma((3, 2)),
        ],
        compiler_params=pltpu.CompilerParams(
            collective_id=0, has_side_effects=True, vmem_limit_bytes=67043328),
        cost_estimate=pl.CostEstimate(flops=flops, bytes_accessed=256 << 20, transcendentals=0),
    )(x_blk, ln_gain.reshape(1, dim), ln_bias.reshape(1, dim), wqkv, w_out, w_up, w_down)
    return outs[:3]


def solution(mesh):
    n_tp = mesh.shape["tp"]

    def local_layer(x_blk, ln_gain, ln_bias, w_qkv, w_out, w_up, w_down):
        dim = x_blk.shape[2]
        wqkv = w_qkv.transpose(0, 2, 1, 3).reshape(dim, -1)
        own, from_left, from_right = layer_call(x_blk, ln_gain, ln_bias, wqkv, w_out, w_up, w_down, n_tp)
        branch = (own.astype(jnp.float32) + from_left.astype(jnp.float32)
                  + from_right.astype(jnp.float32)).astype(jnp.bfloat16)
        return (x_blk.astype(jnp.float32) + branch.astype(jnp.float32)).astype(jnp.bfloat16)

    return jax.shard_map(
        local_layer, mesh=mesh,
        in_specs=(P("dp", "tp", None), P(), P(), P(None, "tp", None, None),
                  P("tp", None), P(None, "tp"), P("tp", None)),
        out_specs=P("dp", "tp", None), check_vma=False)
```

time: 1530 us -> 669 us (0.44)
  matrix products: 781 us -> 0 us
  Pallas kernels: 0 us -> 625 us
  waiting for transfers between devices: 619 us -> 0 us
  other arithmetic: 102 us -> 15.3 us
  local copies, waits for them, and re-layouts: 0.62 us -> 27.3 us
    dot_general x6 -> x0, matrix products: 781 us -> none  [the longest x1 296 us: local_layer(): jnp.einsum('bsf,fd->bsd', activated, w_down, preferred_element_type=jnp.f...]
    pallas_call x0 -> x1, Pallas kernels: none -> 625 us  [layer_call(): pl.pallas_call(layer_kernel, name='parallel_layer', out_shape=[jax.ShapeD...]
    reduce_scatter x1 -> x0, waiting for transfers between devices: 324 us -> none  [local_layer(): lax.psum_scatter(branch_part, 'tp', scatter_dimension=1, tiled=True)]
    all_gather x1 -> x0, waiting for transfers between devices: 294 us -> none  [local_layer(): x_full = lax.all_gather(x_blk, 'tp', axis=1, tiled=True)]
    reduce_sum x3 -> x0, other arithmetic: 87.4 us -> none  [the longest x1 42.4 us: local_layer(): attn_prob = jax.nn.softmax(scores, axis=-1).astype(jnp.bfloat16)]
    reshape x0 -> x1, local copies, waits for them, and re-layouts: none -> 27.3 us  [local_layer(): wqkv = w_qkv.transpose(0, 2, 1, 3).reshape(dim, -1)]
  transfers between devices with their start and end apart: 2 -> 0, of which waited for: 2 -> 0; matrix products, arithmetic and copies ran while one was open for 0% -> 0% of each run, Pallas kernels for 0% -> 0%
where the time goes in v1:
time: 669 us; the launch traced here: 668 us
  Pallas kernels  625 us (93%)
  local copies, waits for them, and re-layouts  27.3 us (4%)
  other arithmetic  15.3 us (2%)
    pallas_call x1, Pallas kernels, layer_call(): pl.pallas_call(layer_kernel, name='parallel_layer', out_shape=[jax.ShapeD...  625 us
    reshape x1, local copies, waits for them, and re-layouts, local_layer(): wqkv = w_qkv.transpose(0, 2, 1, 3).reshape(dim, -1)  27.3 us
    convert_element_type x1, other arithmetic, local_layer(): (x_blk.astype(jnp.float32) + branch.astype(jnp.float32)).astype(jnp.bfloa...  15.3 us

profile of v1, /device:TPU:112, one launch (start us, length us, event | category | flops | bytes accessed | tf_op | source)
XLA Modules:
  0.0 667.5 jit_solution(9678228306904514390)
XLA Ops:
  0.0 27.3 %reshape.11.wqkv_hbm = bf16[4096,1536]{1,0:T(8,128)(2,1)} reshape(bf16[4096,3,2,256]{3,2,1,0:T(2,128)(2,1)} %bitcast.3) | data formatting | bytes 25165824 | tf_op jit(solution)/shard_map/reshape | solution.py:502
  27.3 624.9 %parallel_layer.1 = (bf16[4,256,4096]{2,1,0:T(8,128)(2,1)}, bf16[4,256,4096]{2,1,0:T(8,128)(2,1)}, bf16[4,256,4096]{2,1,0:T(8,128)(2,1)}, bf16[4,4,2,256,4096]{4...) custom-call(bf16[4,256,4096]{2,1,0:T(8,128)(2,1)} %x_ref.1, ...), custom_call_target="tpu_custom_call" | custom-call | flops 412316860416 | bytes 268435456 | tf_op jit(solution)/shard_map/parallel_layer/pallas_call | solution.py:466
  652.2 15.3 %add_convert_fusion = bf16[4,256,4096]{2,1,0:T(8,128)(2,1)} fusion(bf16[4,256,4096]{2,1,0:T(8,128)(2,1)} %x_ref.1, bf16[4,256,4096]{2,1,0:T(8,128)(2,1)} %get-tuple-element.10, bf16[4,256,4096]{2,1,0:T(8,128)(2,1)} %get-tuple-element.9, bf16[4,256,4096]{2,1,0:T(8,128)(2,1)} %get-tuple-element.8), kind=kLoop, calls=%fused_computation | loop fusion | flops 41943040 | bytes 41943040 | tf_op jit(solution)/shard_map/convert_element_type | solution.py:506

commit v2 on v1

--- a/solution.py
+++ b/solution.py
@@ -46,10 +46,9 @@
     pl.semaphore_wait(barrier, 3)
 
     w_copies = (
-        pltpu.make_async_copy(wqkv_hbm, wqkv, w_sem.at[0]),
-        pltpu.make_async_copy(wup_hbm, wup, w_sem.at[1]),
-        pltpu.make_async_copy(wdown_hbm, wdo.at[pl.ds(0, ff)], w_sem.at[2]),
-        pltpu.make_async_copy(wout_hbm, wdo.at[pl.ds(ff, attn)], w_sem.at[3]),
+        pltpu.make_async_copy(wup_hbm, wup, w_sem.at[2]),
+        pltpu.make_async_copy(wdown_hbm, wdo.at[pl.ds(0, ff)], w_sem.at[3]),
+        pltpu.make_async_copy(wout_hbm, wdo.at[pl.ds(ff, attn)], w_sem.at[4]),
     )
     v_copies = (pltpu.make_async_copy(gain_ref, gain, v_sem.at[0]),
                 pltpu.make_async_copy(bias_ref, bias, v_sem.at[1]))
@@ -97,11 +96,14 @@
                 var = jnp.mean(cen * cen, axis=-1, keepdims=True)
                 buf[at, :] = (cen * lax.rsqrt(var + LN_EPS) * gain[...] + bias[...]).astype(bf16)
             store(q).start()
-        for q in range(4):
-            store(q).wait()
-        ici_copy(s, 2, chip, 0, right).start()
+            if q == 1:
+                store(0).wait()
+                store(1).wait()
+                ici_copy(s, 2, chip, 0, right).start()
+                d2d_copy(s, 0, chip, 0, core).start()
+        store(2).wait()
+        store(3).wait()
         ici_copy(s, 3, chip, 1, left).start()
-        d2d_copy(s, 0, chip, 0, core).start()
         d2d_copy(s, 1, chip, 1, core).start()
         ici_copy(s, 4, chip, 1, right).start()
         ici_copy(s, 5, chip, 0, left).start()
@@ -109,7 +111,8 @@
     def forward(s, us):
         for u in us:
             d, hf = unit(u)
-            ici_copy(s, u, d, hf, right).wait_recv()
+            with jax.named_scope(f"ici_wait_{u}"):
+                ici_copy(s, u, d, hf, right).wait_recv()
             if u == 2:
                 ici_copy(s, 6, d, hf, right).start()
             if u == 3:
@@ -149,14 +152,16 @@
             order = tuple(range(NJ))
             for n, j in enumerate(order):
                 if n == 0:
-                    transit(s, j, right).wait_recv()
+                    with jax.named_scope("relay_wait"):
+                        transit(s, j, right).wait_recv()
                     for cp in loads(j):
                         cp.start()
                 if n >= 1:
                     store(order[n - 1]).wait()
                     send(order[n - 1]).start()
                 if n + 1 < NJ:
-                    transit(s, order[n + 1], right).wait_recv()
+                    with jax.named_scope("relay_wait"):
+                        transit(s, order[n + 1], right).wait_recv()
                     for cp in loads(order[n + 1]):
                         cp.start()
                 for cp in loads(j):
@@ -180,7 +185,8 @@
 
             def arrived(u):
                 d, hf = unit(u)
-                d2d_copy(s, u, d, hf, other).wait_recv()
+                with jax.named_scope("d2d_wait"):
+                    d2d_copy(s, u, d, hf, other).wait_recv()
 
             def hstore(u, k):
                 d, hf = unit(u)
@@ -194,7 +200,8 @@
 
             @pl.loop(0, 2 * n_chips)
             def _(u):
-                load(u).wait()
+                with jax.named_scope("load_wait"):
+                    load(u).wait()
 
                 @pl.when(jnp.logical_and(s > 0, u == 3))
                 def _():
@@ -213,7 +220,6 @@
                 @pl.when(jnp.logical_and(s == 0, u == 0))
                 def _():
                     w_copies[0].wait()
-                    w_copies[1].wait()
 
                 d, hf = unit(u)
                 slot = u % 2
@@ -310,7 +316,8 @@
                 return pltpu.make_async_copy(pbuf.at[s, m // NJ, m % NJ], pb.at[m % 2], pb_sem.at[m % 2])
 
             def pb_start(m):
-                swap(m).wait_recv()
+                with jax.named_scope("swap_wait"):
+                    swap(m).wait_recv()
                 pb_load(m).start()
 
             def ostore(m):
@@ -343,8 +350,8 @@
 
             @pl.when(s == 0)
             def _():
+                w_copies[1].wait()
                 w_copies[2].wait()
-                w_copies[3].wait()
             load_p(0).wait()
             load_p(1).start()
             load_o(1).start()
@@ -416,48 +423,85 @@
         pl.run_scoped(scope, pltpu.VMEM((2, 2 * rows, ff + attn), bf16), pltpu.VMEM((2, rows, ncol), bf16),
                       pltpu.VMEM((2, rows, ncol), bf16), pltpu.VMEM((2, rows, ncol), bf16))
 
+    def place_qkv(raw, wide):
+        kinds = qkv_cols // attn
+        per = qkv_cols // 128
+        chunk = raw.shape[1] // per
+        n_chunks = dim // chunk
+
+        def load(q):
+            at = pl.ds(pl.multiple_of(q * (chunk * per), chunk * per), chunk * per)
+            return pltpu.make_async_copy(wqkv_hbm.at[at], raw.at[q % 2], w_sem.at[q % 2])
+
+        load(0).start()
+
+        @pl.loop(0, n_chunks)
+        def _(q):
+            @pl.when(q + 1 < n_chunks)
+            def _():
+                load(q + 1).start()
+            load(q).wait()
+            wide[...] = raw[q % 2].astype(f32)
+            for j in range(kinds):
+                for c in range(head // 128):
+                    for g in range(n_heads):
+                        row = (j * (head // 128) + c) * n_heads + g
+                        col = j * attn + g * head + c * 128
+                        wqkv[pl.ds(pl.multiple_of(q * chunk, chunk), chunk), col:col + 128] = (
+                            wide[pl.ds(row, chunk, stride=per), :].astype(bf16))
+
     for cp in v_copies:
         cp.wait()
-    pl.run_scoped(functools.partial(ag_send, 0), pltpu.VMEM((rows, dim), bf16))
+    with jax.named_scope("send0"):
+        pl.run_scoped(functools.partial(ag_send, 0), pltpu.VMEM((rows, dim), bf16))
     for cp in w_copies:
         cp.start()
+    with jax.named_scope("place"):
+        pl.run_scoped(place_qkv, pltpu.VMEM((2, 128 * (qkv_cols // 128), 128), bf16),
+                      pltpu.VMEM((128 * (qkv_cols // 128), 128), f32))
 
     @pl.loop(0, batch)
     def _(s):
         def scope(qkv):
-            phase_a(s, qkv)
+            with jax.named_scope("A"):
+                phase_a(s, qkv)
 
             @pl.when(s > 0)
             def _():
-                relay(s - 1)
-            phase_b(qkv)
+                with jax.named_scope("relay"):
+                    relay(s - 1)
+            with jax.named_scope("B"):
+                phase_b(qkv)
         pl.run_scoped(scope, pltpu.VMEM((seq, qkv_cols), bf16))
-        phase_d(s)
+        with jax.named_scope("D"):
+            phase_d(s)
 
         @pl.when(s < batch - 2)
         def _():
             pl.run_scoped(functools.partial(ag_send, s + 2), pltpu.VMEM((rows, dim), bf16))
 
-    relay(batch - 1)
+    with jax.named_scope("relay_last"):
+        relay(batch - 1)
 
     @pl.loop(0, batch)
     def _(s):
-        for j in range(NJ):
-            to_right(s, 1, j).wait_recv()
-            to_left(s, 2, j).wait_recv()
-            to_right(s, 1, j).wait_send()
-            to_left(s, 2, j).wait_send()
-            transit(s, j, right).wait_send()
-        for u in range(2 * n_chips):
-            d, hf = unit(u)
-            d2d_copy(s, u, d, hf, core).wait_send()
-            if u >= 2:
-                ici_copy(s, u, d, hf, right).wait_send()
+        with jax.named_scope("final"):
+            for j in range(NJ):
+                to_right(s, 1, j).wait_recv()
+                to_left(s, 2, j).wait_recv()
+                to_right(s, 1, j).wait_send()
+                to_left(s, 2, j).wait_send()
+                transit(s, j, right).wait_send()
+            for u in range(2 * n_chips):
+                d, hf = unit(u)
+                d2d_copy(s, u, d, hf, core).wait_send()
+                if u >= 2:
+                    ici_copy(s, u, d, hf, right).wait_send()
 
 
 def layer_call(x_blk, ln_gain, ln_bias, wqkv, w_out, w_up, w_down, n_tp):
     batch, rows, dim = x_blk.shape
-    ff, attn, qkv_cols = w_up.shape[1], w_out.shape[0], wqkv.shape[1]
+    ff, attn, qkv_cols = w_up.shape[1], w_out.shape[0], wqkv.shape[0] * 128 // dim
     n_chips = n_tp // 2
     ncol = dim // NJ
     bf16 = jnp.bfloat16
@@ -484,7 +528,7 @@
             dma((batch, 8)), dma((batch, 8)), dma((batch, 8)), dma((batch, 8)),
             dma((2,)), dma((batch, 4 * NJ)), dma((batch, NJ)), dma((batch, NJ)),
             dma((batch, 2 * NJ)), dma((batch, 2 * NJ)),
-            dma((4,)), dma((2,)), dma((2, 4)), dma((2,)), dma((2, 2)), dma((n_tp,)), dma((2, 2)), dma((2,)), dma((2,)),
+            dma((5,)), dma((2,)), dma((2, 4)), dma((2,)), dma((2, 2)), dma((n_tp,)), dma((2, 2)), dma((2,)), dma((2,)),
             dma((3, 2)),
         ],
         compiler_params=pltpu.CompilerParams(
@@ -499,7 +543,8 @@
 
     def local_layer(x_blk, ln_gain, ln_bias, w_qkv, w_out, w_up, w_down):
         dim = x_blk.shape[2]
-        wqkv = w_qkv.transpose(0, 2, 1, 3).reshape(dim, -1)
+        groups, kinds, head = w_qkv.shape[1:]
+        wqkv = w_qkv.reshape(dim, groups, kinds, head // 128, 128).transpose(0, 2, 3, 1, 4).reshape(-1, 128)
         own, from_left, from_right = layer_call(x_blk, ln_gain, ln_bias, wqkv, w_out, w_up, w_down, n_tp)
         branch = (own.astype(jnp.float32) + from_left.astype(jnp.float32)
                   + from_right.astype(jnp.float32)).astype(jnp.bfloat16)

time: 669 us -> 659 us (0.985)
  local copies, waits for them, and re-layouts: 27.3 us -> 0 us
  Pallas kernels: 625 us -> 643 us
    reshape x1 -> x0, local copies, waits for them, and re-layouts: 27.3 us -> none  [local_layer(): wqkv = w_qkv.transpose(0, 2, 1, 3).reshape(dim, -1)]
    pallas_call x1, Pallas kernels: 625 us -> 643 us  [layer_call(): pl.pallas_call(layer_kernel, name='parallel_layer', out_shape=[jax.ShapeD...]
where the time goes in v2:
time: 659 us; the launch traced here: 658 us
  Pallas kernels  643 us (98%)
  other arithmetic  15.3 us (2%)
    pallas_call x1, Pallas kernels, layer_call(): pl.pallas_call(layer_kernel, name='parallel_layer', out_shape=[jax.ShapeD...  643 us
    convert_element_type x1, other arithmetic, local_layer(): (x_blk.astype(jnp.float32) + branch.astype(jnp.float32)).astype(jnp.bfloa...  15.3 us

profile of v2, /device:TPU:112, one launch (start us, length us, event | category | flops | bytes accessed | tf_op | source)
XLA Modules:
  0.0 657.9 jit_solution(14394644789717752627)
XLA Ops:
  0.0 642.6 %parallel_layer.1 = (bf16[4,256,4096]{2,1,0:T(8,128)(2,1)}, bf16[4,256,4096]{2,1,0:T(8,128)(2,1)}, bf16[4,256,4096]{2,1,0:T(8,128)(2,1)}, bf16[4,4,2,256,4096]{4...) custom-call(bf16[4,256,4096]{2,1,0:T(8,128)(2,1)} %x_ref.1, ...), custom_call_target="tpu_custom_call" | custom-call | flops 412316860416 | bytes 268435456 | tf_op jit(solution)/shard_map/parallel_layer/pallas_call | solution.py:510
  642.6 15.3 %add_convert_fusion = bf16[4,256,4096]{2,1,0:T(8,128)(2,1)} fusion(bf16[4,256,4096]{2,1,0:T(8,128)(2,1)} %x_ref.1, bf16[4,256,4096]{2,1,0:T(8,128)(2,1)} %get-tuple-element.10, bf16[4,256,4096]{2,1,0:T(8,128)(2,1)} %get-tuple-element.9, bf16[4,256,4096]{2,1,0:T(8,128)(2,1)} %get-tuple-element.8), kind=kLoop, calls=%fused_computation | loop fusion | flops 41943040 | bytes 41943040 | tf_op jit(solution)/shard_map/convert_element_type | solution.py:551

commit v3 on v2

--- a/solution.py
+++ b/solution.py
@@ -1,5 +1,3 @@
-import functools
-
 import jax
 import jax.numpy as jnp
 from jax import lax
@@ -8,6 +6,7 @@
 from jax.sharding import PartitionSpec as P
 
 LN_EPS = 1e-5
+LOG2_E = 1.4426950408889634
 NJ = 4
 
 
@@ -46,9 +45,9 @@
     pl.semaphore_wait(barrier, 3)
 
     w_copies = (
-        pltpu.make_async_copy(wup_hbm, wup, w_sem.at[2]),
-        pltpu.make_async_copy(wdown_hbm, wdo.at[pl.ds(0, ff)], w_sem.at[3]),
-        pltpu.make_async_copy(wout_hbm, wdo.at[pl.ds(ff, attn)], w_sem.at[4]),
+        pltpu.make_async_copy(wup_hbm, wup, w_sem.at[0]),
+        pltpu.make_async_copy(wdown_hbm, wdo.at[pl.ds(0, ff)], w_sem.at[1]),
+        pltpu.make_async_copy(wout_hbm, wdo.at[pl.ds(ff, attn)], w_sem.at[2]),
     )
     v_copies = (pltpu.make_async_copy(gain_ref, gain, v_sem.at[0]),
                 pltpu.make_async_copy(bias_ref, bias, v_sem.at[1]))
@@ -71,38 +70,50 @@
     def d2d_copy(s, u, d, hf, k):
         return remote(piece(s, d, hf, k), piece(s, d, hf, k), ag_ds.at[s, u], ag_dr.at[s, u], partner)
 
-    def ag_send(s, buf):
-        part, step = rows // 4, 32
-
-        def load(q):
-            at = pl.ds(q * part, part)
-            return pltpu.make_async_copy(x_ref.at[s, at], buf.at[at], ln_sem.at[0, q])
-
-        def store(q):
-            dst = n_all.at[s, chip, q // 2, pl.ds(pl.multiple_of(core * half + (q % 2) * part, part), part)]
-            return pltpu.make_async_copy(buf.at[pl.ds(q * part, part)], dst, ln_sem.at[1, q])
-
+    part = rows // 4
+
+    def x_load(s, buf, q):
+        at = pl.ds(q * part, part)
+        return pltpu.make_async_copy(x_ref.at[s, at], buf.at[at], ln_sem.at[0, q])
+
+    def n_store(s, buf, q):
+        dst = n_all.at[s, chip, q // 2, pl.ds(pl.multiple_of(core * half + (q % 2) * part, part), part)]
+        return pltpu.make_async_copy(buf.at[pl.ds(q * part, part)], dst, ln_sem.at[1, q])
+
+    def x_start(s, buf):
         for q in range(4):
-            load(q).start()
-        for q in range(4):
-            load(q).wait()
-
-            @pl.loop(0, part // step)
-            def _(r):
-                at = pl.ds(pl.multiple_of(q * part + r * step, step), step)
-                v = buf[at, :].astype(f32)
-                mean = jnp.mean(v, axis=-1, keepdims=True)
-                cen = v - mean
-                var = jnp.mean(cen * cen, axis=-1, keepdims=True)
-                buf[at, :] = (cen * lax.rsqrt(var + LN_EPS) * gain[...] + bias[...]).astype(bf16)
-            store(q).start()
-            if q == 1:
-                store(0).wait()
-                store(1).wait()
-                ici_copy(s, 2, chip, 0, right).start()
-                d2d_copy(s, 0, chip, 0, core).start()
-        store(2).wait()
-        store(3).wait()
+            x_load(s, buf, q).start()
+
+    def normalise(s, buf, q):
+        x_load(s, buf, q).wait()
+        at = pl.ds(q * part, part)
+        lanes, wide = 128, 512
+        total = jnp.zeros((part, lanes), f32)
+        for c in range(0, dim, wide):
+            v = buf[at, c:c + wide].astype(f32)
+            for k in range(0, wide, lanes):
+                total = total + v[:, k:k + lanes]
+        mean = jnp.sum(total, axis=-1, keepdims=True) * (1.0 / dim)
+        total = jnp.zeros((part, lanes), f32)
+        for c in range(0, dim, wide):
+            cen = buf[at, c:c + wide].astype(f32) - mean
+            for k in range(0, wide, lanes):
+                total = total + cen[:, k:k + lanes] * cen[:, k:k + lanes]
+        inv = lax.rsqrt(jnp.sum(total, axis=-1, keepdims=True) * (1.0 / dim) + LN_EPS)
+        for c in range(0, dim, wide):
+            cen = buf[at, c:c + wide].astype(f32) - mean
+            buf[at, c:c + wide] = (cen * inv * gain[:, c:c + wide] + bias[:, c:c + wide]).astype(bf16)
+        n_store(s, buf, q).start()
+
+    def send_first(s, buf):
+        n_store(s, buf, 0).wait()
+        n_store(s, buf, 1).wait()
+        ici_copy(s, 2, chip, 0, right).start()
+        d2d_copy(s, 0, chip, 0, core).start()
+
+    def send_rest(s, buf):
+        n_store(s, buf, 2).wait()
+        n_store(s, buf, 3).wait()
         ici_copy(s, 3, chip, 1, left).start()
         d2d_copy(s, 1, chip, 1, core).start()
         ici_copy(s, 4, chip, 1, right).start()
@@ -137,48 +148,59 @@
     def transit(s, j, dev):
         return remote(pout.at[s, 0, :, cols(j)], tin.at[s, :, cols(j)], t_s.at[s, j], t_r.at[s, j], dev)
 
-    def relay(s):
+    def relay_loads(s, q, k, a, b):
+        return (pltpu.make_async_copy(pout.at[s, 1 + q // 2, :, cols(q)], a, f_sem.at[0, k]),
+                pltpu.make_async_copy(tin.at[s, :, cols(q)], b, f_sem.at[1, k]))
+
+    def relay_store(s, q, k, a):
+        return pltpu.make_async_copy(a, pout.at[s, 1 + q // 2, :, cols(q)], f_sem.at[2, k])
+
+    def relay_start(s, q, k, a, b):
+        transit(s, q, right).wait_recv()
+        for cp in relay_loads(s, q, k, a, b):
+            cp.start()
+
+    def relay_add(s, q, k, a, b):
+        for cp in relay_loads(s, q, k, a, b):
+            cp.wait()
+        step = 64
+
+        @pl.loop(0, rows // step)
+        def _(r):
+            at = pl.ds(pl.multiple_of(r * step, step), step)
+            a[at, :] = (a[at, :].astype(f32) + b[at, :].astype(f32)).astype(bf16)
+        relay_store(s, q, k, a).start()
+
+    def relay_send(s, q, k, a):
+        relay_store(s, q, k, a).wait()
+
+        @pl.when(q < NJ // 2)
+        def _():
+            to_right(s, 1, q).start()
+
+        @pl.when(q >= NJ // 2)
+        def _():
+            to_left(s, 2, q).start()
+
+    def relay_all(s):
         def scope(a, b):
-            def loads(j):
-                return (pltpu.make_async_copy(pout.at[s, 1 + j // 2, :, cols(j)], a.at[j % 2], f_sem.at[0, j % 2]),
-                        pltpu.make_async_copy(tin.at[s, :, cols(j)], b.at[j % 2], f_sem.at[1, j % 2]))
-
-            def store(j):
-                return pltpu.make_async_copy(a.at[j % 2], pout.at[s, 1 + j // 2, :, cols(j)], f_sem.at[2, j % 2])
-
-            def send(j):
-                return to_right(s, 1, j) if j < NJ // 2 else to_left(s, 2, j)
-
-            order = tuple(range(NJ))
-            for n, j in enumerate(order):
-                if n == 0:
-                    with jax.named_scope("relay_wait"):
-                        transit(s, j, right).wait_recv()
-                    for cp in loads(j):
-                        cp.start()
-                if n >= 1:
-                    store(order[n - 1]).wait()
-                    send(order[n - 1]).start()
+            order = (0, 2, 1, 3)
+
+            def bufs(n):
+                return n % 2, a.at[n % 2], b.at[n % 2]
+            relay_start(s, order[0], *bufs(0))
+            for n in range(NJ):
                 if n + 1 < NJ:
-                    with jax.named_scope("relay_wait"):
-                        transit(s, order[n + 1], right).wait_recv()
-                    for cp in loads(order[n + 1]):
-                        cp.start()
-                for cp in loads(j):
-                    cp.wait()
-                step = 64
-
-                @pl.loop(0, rows // step)
-                def _(r):
-                    at = pl.ds(pl.multiple_of(r * step, step), step)
-                    a[j % 2, at, :] = (a[j % 2, at, :].astype(f32) + b[j % 2, at, :].astype(f32)).astype(bf16)
-                store(j).start()
-            store(order[-1]).wait()
-            send(order[-1]).start()
+                    if n >= 1:
+                        relay_send(s, order[n - 1], *bufs(n - 1)[:2])
+                    relay_start(s, order[n + 1], *bufs(n + 1))
+                relay_add(s, order[n], *bufs(n))
+            for n in (NJ - 2, NJ - 1):
+                relay_send(s, order[n], *bufs(n)[:2])
         pl.run_scoped(scope, pltpu.VMEM((2, rows, ncol), bf16), pltpu.VMEM((2, rows, ncol), bf16))
 
     def phase_a(s, qkv):
-        def scope(nbuf, hbuf):
+        def scope(nbuf, hbuf, ra, rb):
             def load(u):
                 d, hf = unit(u)
                 return pltpu.make_async_copy(n_all.at[s, d, hf], nbuf.at[u % 2], a_sem.at[u % 2])
@@ -191,9 +213,9 @@
             def hstore(u, k):
                 d, hf = unit(u)
                 return pltpu.make_async_copy(
-                    hbuf.at[u % 2, pl.ds(k * half, half)],
+                    hbuf.at[pl.ds(k * half, half)],
                     ho.at[2 * d + k, pl.ds(pl.multiple_of(hf * half, half), half), pl.ds(0, ff)],
-                    h_sem.at[u % 2, k])
+                    h_sem.at[k])
 
             arrived(0)
             load(0).start()
@@ -207,15 +229,26 @@
                 def _():
                     forward(s, (6, 7))
 
-                @pl.when(jnp.logical_and(s > 0, u < 7))
+                @pl.when(jnp.logical_or(jnp.logical_and(s > 0, u < 7), u % 2 == 0))
                 def _():
                     arrived(u + 1)
                     load(u + 1).start()
 
-                @pl.when(u >= 2)
-                def _():
-                    for k in range(2):
-                        hstore(u - 2, k).wait()
+                @pl.when(jnp.logical_and(s == 0, u == 1))
+                def _():
+                    x_start(1, nbuf.at[0])
+
+                @pl.when(jnp.logical_and(s > 0, jnp.logical_and(u >= 3, u % 2 == 1)))
+                def _():
+                    relay_send(s - 1, (u - 3) // 2, 0, ra)
+
+                @pl.when(jnp.logical_and(s > 0, u % 2 == 1))
+                def _():
+                    relay_start(s - 1, (u - 1) // 2, 0, ra, rb)
+
+                @pl.when(jnp.logical_and(s > 0, jnp.logical_and(u >= 2, u % 2 == 0)))
+                def _():
+                    relay_add(s - 1, (u - 2) // 2, 0, ra, rb)
 
                 @pl.when(jnp.logical_and(s == 0, u == 0))
                 def _():
@@ -227,8 +260,13 @@
                 for k in range(2):
                     pos = pl.multiple_of(d * (2 * rows) + k * rows + hf * half, half)
                     qkv[pl.ds(pos, half), :] = r[k * half:(k + 1) * half]
+
+                @pl.when(u >= 1)
+                def _():
+                    for k in range(2):
+                        hstore(u - 1, k).wait()
                 h = jnp.dot(nbuf[slot], wup[...], preferred_element_type=f32)
-                hbuf[slot] = (0.5 * h * (1.0 + lax.erf(h * (2.0 ** -0.5)))).astype(bf16)
+                hbuf[...] = (0.5 * h * (1.0 + lax.erf(h * (2.0 ** -0.5)))).astype(bf16)
                 for k in range(2):
                     hstore(u, k).start()
 
@@ -237,7 +275,11 @@
                     @pl.when(u == 1)
                     def _():
                         forward(0, (2, 3))
-                        ag_send(1, nbuf.at[0])
+                        with jax.named_scope("send1"):
+                            for q in range(4):
+                                normalise(1, nbuf.at[0], q)
+                            send_first(1, nbuf.at[0])
+                            send_rest(1, nbuf.at[0])
 
                     @pl.when(u == 3)
                     def _():
@@ -247,15 +289,20 @@
                     def _():
                         forward(0, (6, 7))
 
-                    @pl.when(u < 7)
+                    @pl.when(jnp.logical_and(u < 7, u % 2 == 1))
                     def _():
                         arrived(u + 1)
                         load(u + 1).start()
 
-            for u in (6, 7):
-                for k in range(2):
-                    hstore(u, k).wait()
-        pl.run_scoped(scope, pltpu.VMEM((2, rows, dim), bf16), pltpu.VMEM((2, rows, ff), bf16))
+            @pl.when(s > 0)
+            def _():
+                with jax.named_scope("relay_end"):
+                    relay_add(s - 1, NJ - 1, 0, ra, rb)
+                    relay_send(s - 1, NJ - 1, 0, ra)
+            for k in range(2):
+                hstore(7, k).wait()
+        pl.run_scoped(scope, pltpu.VMEM((2, rows, dim), bf16), pltpu.VMEM((rows, ff), bf16),
+                      pltpu.VMEM((rows, ncol), bf16), pltpu.VMEM((rows, ncol), bf16))
 
     def phase_b(qkv):
         def ostore(t):
@@ -266,41 +313,57 @@
         def scope(scores, probs):
             keep = (lax.broadcasted_iota(jnp.int32, (rows, rows), 0)
                     >= lax.broadcasted_iota(jnp.int32, (rows, rows), 1))
-            for t in range(seq // rows):
+            tasks = [(t, h) for t in range(seq // rows) for h in range(n_heads)]
+            tops = {}
+
+            def score(i):
+                t, h = tasks[i]
                 r0, n = t * rows, (t + 1) * rows
-                tops = []
-                for h in range(n_heads):
-                    q = qkv[r0:r0 + rows, h * head:(h + 1) * head]
-                    k = qkv[0:n, attn + h * head:attn + (h + 1) * head]
-                    sc = lax.dot_general(q, k, (((1,), (1,)), ((), ())), preferred_element_type=f32)
-                    diag = jnp.where(keep, sc[:, n - rows:], -jnp.inf)
-                    top = jnp.max(diag, axis=1, keepdims=True)
-                    if t:
-                        scores[h, :, 0:n - rows] = sc[:, :n - rows]
-                        top = jnp.maximum(top, jnp.max(sc[:, :n - rows], axis=1, keepdims=True))
-                    scores[h, :, n - rows:n] = diag
-                    tops.append(top)
-                for h in range(n_heads):
-                    v = qkv[0:n, 2 * attn + h * head:2 * attn + (h + 1) * head]
-                    total = jnp.zeros((rows, 1), f32)
-                    for c in range(0, n, rows):
-                        e = jnp.exp((scores[h, :, c:c + rows] - tops[h]) * scale)
-                        scores[h, :, c:c + rows] = e
-                        total = total + jnp.sum(e, axis=1, keepdims=True)
-                    inverse = 1.0 / total
-                    for c in range(0, n, rows):
-                        probs[h, :, c:c + rows] = (scores[h, :, c:c + rows] * inverse).astype(bf16)
-                    o = jnp.dot(probs[h, :, 0:n], v, preferred_element_type=f32)
-                    qkv[r0:r0 + rows, h * head:(h + 1) * head] = o.astype(bf16)
-                if t % 4 == 3:
-                    for done in range(t - 3, t + 1):
+                q = qkv[r0:n, h * head:(h + 1) * head]
+                k = qkv[0:n, attn + h * head:attn + (h + 1) * head]
+                sc = lax.dot_general(q, k, (((1,), (1,)), ((), ())), preferred_element_type=f32)
+                diag = jnp.where(keep, sc[:, r0:], -jnp.inf)
+                top = jnp.max(diag, axis=1, keepdims=True)
+                if t:
+                    scores[i % 2, :, 0:r0] = sc[:, :r0]
+                    top = jnp.maximum(top, jnp.max(sc[:, :r0], axis=1, keepdims=True))
+                scores[i % 2, :, r0:n] = diag
+                tops[i] = top
+
+            def soften(i):
+                t, h = tasks[i]
+                n = (t + 1) * rows
+                total = jnp.zeros((rows, rows // 2), f32)
+                for c in range(0, n, rows):
+                    e = jnp.exp2((scores[i % 2, :, c:c + rows] - tops[i]) * (scale * LOG2_E))
+                    scores[i % 2, :, c:c + rows] = e
+                    total = total + e[:, :rows // 2] + e[:, rows // 2:]
+                inverse = 1.0 / jnp.sum(total, axis=1, keepdims=True)
+                for c in range(0, n, rows):
+                    probs[i % 2, :, c:c + rows] = (scores[i % 2, :, c:c + rows] * inverse).astype(bf16)
+
+            def mix(i):
+                t, h = tasks[i]
+                r0, n = t * rows, (t + 1) * rows
+                v = qkv[0:n, 2 * attn + h * head:2 * attn + (h + 1) * head]
+                o = jnp.dot(probs[i % 2, :, 0:n], v, preferred_element_type=f32)
+                qkv[r0:n, h * head:(h + 1) * head] = o.astype(bf16)
+
+            score(0)
+            for i in range(len(tasks)):
+                if i + 1 < len(tasks):
+                    score(i + 1)
+                soften(i)
+                mix(i)
+                if i % n_heads == n_heads - 1 and tasks[i][0] % 4 == 3:
+                    for done in range(tasks[i][0] - 3, tasks[i][0] + 1):
                         ostore(done).start()
             for t in range(seq // rows):
                 ostore(t).wait()
         pl.run_scoped(scope, pltpu.VMEM((n_heads, rows, seq), f32), pltpu.VMEM((n_heads, rows, seq), bf16))
 
     def phase_d(s):
-        def scope(lhs, pst, ost, pb):
+        def scope(lhs, pst, ost, pb, xbuf):
             def load_p(i):
                 return pltpu.make_async_copy(ho.at[2 * dest(i) + other], lhs.at[i % 2, pl.ds(0, rows)],
                                              d_sem.at[i % 2, 0])
@@ -355,6 +418,10 @@
             load_p(0).wait()
             load_p(1).start()
             load_o(1).start()
+
+            @pl.when(s < batch - 2)
+            def _():
+                x_start(s + 2, xbuf)
 
             @pl.loop(0, NJ)
             def _(j):
@@ -403,6 +470,12 @@
             @pl.when(s < batch - 1)
             def _():
                 forward(s + 1, (4, 5))
+
+            @pl.when(s < batch - 2)
+            def _():
+                with jax.named_scope("norm2"):
+                    for q in range(4):
+                        normalise(s + 2, xbuf, q)
             load_o(4).wait()
 
             @pl.loop(3 * NJ, 4 * NJ)
@@ -420,45 +493,58 @@
             ostored(4 * NJ - 1)
             for p in (4 * NJ - 2, 4 * NJ - 1):
                 swap(p).wait_send()
+
+            @pl.when(s < batch - 2)
+            def _():
+                send_first(s + 2, xbuf)
+                send_rest(s + 2, xbuf)
         pl.run_scoped(scope, pltpu.VMEM((2, 2 * rows, ff + attn), bf16), pltpu.VMEM((2, rows, ncol), bf16),
-                      pltpu.VMEM((2, rows, ncol), bf16), pltpu.VMEM((2, rows, ncol), bf16))
-
-    def place_qkv(raw, wide):
+                      pltpu.VMEM((2, rows, ncol), bf16), pltpu.VMEM((2, rows, ncol), bf16),
+                      pltpu.VMEM((rows, dim), bf16))
+
+    def opening(raw, wide, xbuf):
         kinds = qkv_cols // attn
         per = qkv_cols // 128
-        chunk = raw.shape[1] // per
-        n_chunks = dim // chunk
+        n_parts = 8
+        piece_rows = raw.shape[0] // n_parts
+        chunk = wide.shape[0] // per
 
         def load(q):
-            at = pl.ds(pl.multiple_of(q * (chunk * per), chunk * per), chunk * per)
-            return pltpu.make_async_copy(wqkv_hbm.at[at], raw.at[q % 2], w_sem.at[q % 2])
-
-        load(0).start()
-
-        @pl.loop(0, n_chunks)
-        def _(q):
-            @pl.when(q + 1 < n_chunks)
-            def _():
-                load(q + 1).start()
-            load(q).wait()
-            wide[...] = raw[q % 2].astype(f32)
-            for j in range(kinds):
-                for c in range(head // 128):
-                    for g in range(n_heads):
-                        row = (j * (head // 128) + c) * n_heads + g
-                        col = j * attn + g * head + c * 128
-                        wqkv[pl.ds(pl.multiple_of(q * chunk, chunk), chunk), col:col + 128] = (
-                            wide[pl.ds(row, chunk, stride=per), :].astype(bf16))
-
-    for cp in v_copies:
-        cp.wait()
-    with jax.named_scope("send0"):
-        pl.run_scoped(functools.partial(ag_send, 0), pltpu.VMEM((rows, dim), bf16))
-    for cp in w_copies:
-        cp.start()
-    with jax.named_scope("place"):
-        pl.run_scoped(place_qkv, pltpu.VMEM((2, 128 * (qkv_cols // 128), 128), bf16),
-                      pltpu.VMEM((128 * (qkv_cols // 128), 128), f32))
+            at = pl.ds(q * piece_rows, piece_rows)
+            return pltpu.make_async_copy(wqkv_hbm.at[at], raw.at[at], o_sem.at[q])
+
+        x_start(0, xbuf)
+        for q in range(n_parts):
+            load(q).start()
+        w_copies[0].start()
+        for cp in v_copies:
+            cp.wait()
+        with jax.named_scope("send0"):
+            normalise(0, xbuf, 0)
+            normalise(0, xbuf, 1)
+            send_first(0, xbuf)
+            normalise(0, xbuf, 2)
+            normalise(0, xbuf, 3)
+            send_rest(0, xbuf)
+        with jax.named_scope("place"):
+            for q in range(n_parts):
+                load(q).wait()
+
+            @pl.loop(0, dim // chunk)
+            def _(q):
+                wide[...] = raw[pl.ds(pl.multiple_of(q * (chunk * per), chunk * per), chunk * per), :].astype(f32)
+                for j in range(kinds):
+                    for c in range(head // 128):
+                        for g in range(n_heads):
+                            row = (j * (head // 128) + c) * n_heads + g
+                            col = j * attn + g * head + c * 128
+                            wqkv[pl.ds(pl.multiple_of(q * chunk, chunk), chunk), col:col + 128] = (
+                                wide[pl.ds(row, chunk, stride=per), :].astype(bf16))
+        for cp in w_copies[1:]:
+            cp.start()
+
+    pl.run_scoped(opening, pltpu.VMEM((dim * (qkv_cols // 128), 128), bf16),
+                  pltpu.VMEM((128 * (qkv_cols // 128), 128), f32), pltpu.VMEM((rows, dim), bf16))
 
     @pl.loop(0, batch)
     def _(s):
@@ -466,22 +552,14 @@
             with jax.named_scope("A"):
                 phase_a(s, qkv)
 
-            @pl.when(s > 0)
-            def _():
-                with jax.named_scope("relay"):
-                    relay(s - 1)
             with jax.named_scope("B"):
                 phase_b(qkv)
         pl.run_scoped(scope, pltpu.VMEM((seq, qkv_cols), bf16))
         with jax.named_scope("D"):
             phase_d(s)
 
-        @pl.when(s < batch - 2)
-        def _():
-            pl.run_scoped(functools.partial(ag_send, s + 2), pltpu.VMEM((rows, dim), bf16))
-
     with jax.named_scope("relay_last"):
-        relay(batch - 1)
+        relay_all(batch - 1)
 
     @pl.loop(0, batch)
     def _(s):
@@ -528,7 +606,7 @@
             dma((batch, 8)), dma((batch, 8)), dma((batch, 8)), dma((batch, 8)),
             dma((2,)), dma((batch, 4 * NJ)), dma((batch, NJ)), dma((batch, NJ)),
             dma((batch, 2 * NJ)), dma((batch, 2 * NJ)),
-            dma((5,)), dma((2,)), dma((2, 4)), dma((2,)), dma((2, 2)), dma((n_tp,)), dma((2, 2)), dma((2,)), dma((2,)),
+            dma((3,)), dma((2,)), dma((2, 4)), dma((2,)), dma((2,)), dma((n_tp,)), dma((2, 2)), dma((2,)), dma((2,)),
             dma((3, 2)),
         ],
         compiler_params=pltpu.CompilerParams(

time: 659 us -> 606 us (0.920)
  Pallas kernels: 643 us -> 590 us
    pallas_call x1, Pallas kernels: 643 us -> 590 us  [layer_call(): pl.pallas_call(layer_kernel, name='parallel_layer', out_shape=[jax.ShapeD...]
where the time goes in v3:
time: 606 us; the launch traced here: 605 us
  Pallas kernels  590 us (97%)
  other arithmetic  15.3 us (3%)
    pallas_call x1, Pallas kernels, layer_call(): pl.pallas_call(layer_kernel, name='parallel_layer', out_shape=[jax.ShapeD...  590 us
    convert_element_type x1, other arithmetic, local_layer(): (x_blk.astype(jnp.float32) + branch.astype(jnp.float32)).astype(jnp.bfloa...  15.3 us

profile of v3, /device:TPU:112, one launch (start us, length us, event | category | flops | bytes accessed | tf_op | source)
XLA Modules:
  0.0 605.4 jit_solution(431733466691508420)
XLA Ops:
  0.0 590.1 %parallel_layer.1 = (bf16[4,256,4096]{2,1,0:T(8,128)(2,1)}, bf16[4,256,4096]{2,1,0:T(8,128)(2,1)}, bf16[4,256,4096]{2,1,0:T(8,128)(2,1)}, bf16[4,4,2,256,4096]{4...) custom-call(bf16[4,256,4096]{2,1,0:T(8,128)(2,1)} %x_ref.1, ...), custom_call_target="tpu_custom_call" | custom-call | flops 412316860416 | bytes 268435456 | tf_op jit(solution)/shard_map/parallel_layer/pallas_call | solution.py:588
  590.1 15.3 %add_convert_fusion = bf16[4,256,4096]{2,1,0:T(8,128)(2,1)} fusion(bf16[4,256,4096]{2,1,0:T(8,128)(2,1)} %x_ref.1, bf16[4,256,4096]{2,1,0:T(8,128)(2,1)} %get-tuple-element.10, bf16[4,256,4096]{2,1,0:T(8,128)(2,1)} %get-tuple-element.9, bf16[4,256,4096]{2,1,0:T(8,128)(2,1)} %get-tuple-element.8), kind=kLoop, calls=%fused_computation | loop fusion | flops 41943040 | bytes 41943040 | tf_op jit(solution)/shard_map/convert_element_type | solution.py:629
